TPU v7x, 32 devices: a whole 2x2x4 slice. The times are simulated.
32 devices in a mesh: dp: 8 (over z, y), tensor: 4 (over x, core).
Axes of the slice: x: 2, y: 2, z: 4, core: 2. Of those that a mesh axis runs over, the one named last changes fastest.
Arguments:
- hidden: bfloat16 [2048, 18432], P('dp', 'tensor'), may hold values from -6 to 6
- down_weight: bfloat16 [18432, 4608], P('tensor', 'dp'), may hold values from -0.046875 to 0.046875
- residual: bfloat16 [2048, 4608], P('dp'), may hold values from -6 to 6
- post_gain: float32 [4608], replicated, may hold values from 0.5 to 1.5
- pre_gain: float32 [4608], replicated, may hold values from 0.5 to 1.5
- cast_scale: float32 [1], replicated, may hold values from 100 to 400
- amax_history: float32 [3, 1024], replicated, may hold values from 0.25 to 4
Outputs:
- cast_out: bfloat16 [2048, 4608], P('dp')
- residual_out: bfloat16 [2048, 4608], P('dp')
- peaks: float32 [3], replicated
- new_history: float32 [3, 1024], replicated
- new_scales: float32 [3], replicated
All inputs are finite; a program needn't handle non-finite values.
Results may differ from a plain program's by a relative error of at most 0.012.
Values may be sent and summed in bfloat16 or wider, within the bound.
No kernel may reach another device: no remote copies, remote signals or barrier semaphores. Data moves between devices by JAX's collectives and lax.ppermute only.
A program may use at most 128 MiB of HBM per device.

v0:
```python
import jax
import jax.numpy as jnp
from jax import lax
from jax.sharding import PartitionSpec as P

norm_epsilon = 1e-06
float_limit = 448.0


def rms_norm(values, gain_vector):
    return (
        values
        * lax.rsqrt(jnp.mean(values * values, axis=-1, keepdims=True) + norm_epsilon)
        * gain_vector
    )


def finish(summed, stream_in, post_gain, pre_gain, stale_scale):
    stream = stream_in.astype(jnp.float32) + rms_norm(summed, post_gain)
    normed = rms_norm(stream, pre_gain)
    cast_rows = (jnp.clip(normed * stale_scale, -float_limit, float_limit) / stale_scale).astype(
        jnp.bfloat16
    )
    peak_values = jnp.stack(
        [jnp.max(jnp.abs(summed)), jnp.max(jnp.abs(stream)), jnp.max(jnp.abs(normed))]
    )
    return (cast_rows, stream.astype(jnp.bfloat16), peak_values)


def on_device(hidden, down_weight, residual, post_gain, pre_gain, cast_scale, amax_history):
    stale_scale = cast_scale[0]
    partial_value = jnp.dot(
        lax.all_gather(hidden, "dp", axis=0, tiled=True),
        down_weight,
        preferred_element_type=jnp.float32,
    )
    column_total = lax.psum(partial_value.astype(jnp.bfloat16), "tensor").astype(jnp.float32)
    summed = lax.all_to_all(
        column_total.astype(jnp.bfloat16), "dp", split_axis=0, concat_axis=1, tiled=True
    ).astype(column_total.dtype)
    cast_out, residual_out, peak_values = finish(summed, residual, post_gain, pre_gain, stale_scale)
    peak_values = lax.pmax(peak_values, ("dp", "tensor"))
    new_history = jnp.concatenate([peak_values[:, None], amax_history[:, :-1]], axis=1)
    new_scales = float_limit / jnp.maximum(jnp.max(new_history, axis=1), 1.0)
    return (cast_out, residual_out, peak_values, new_history, new_scales)


def solution(mesh):
    in_specs = (P("dp", "tensor"), P("tensor", "dp"), P("dp", None), P(), P(), P(), P())
    out_specs = (P("dp", None), P("dp", None), P(), P(), P())
    return jax.shard_map(
        on_device, mesh=mesh, in_specs=in_specs, out_specs=out_specs, check_vma=False
    )
```

profile of v0, /device:TPU:10, one launch (start us, length us, event | category | flops | bytes accessed | tf_op | source)
XLA Modules:
  0.0 571.8 jit_solution(3271551437250830169)
XLA Ops:
  7.2 0.0 all-gather.2.cloned.1.call-start
  7.2 0.7 all-gather.2.cloned.1.call-update
  7.9 0.0 all-reduce.2.cloned.1.call-start
  7.9 365.1 %all-gather.2.cloned.1.call-done = bf16[2048,4608]{1,0:T(8,128)(2,1)} async-done(((bf16[256,4608]{1,0:T(8,128)(2,1)}), bf16[2048,4608]{1,0:T(8,128)(2,1)}) %all-gather.2.cloned.1.call-update) | async-done | bytes 18874384 | tf_op jit(solution)/shard_map/all_gather | solution.py:33
  373.0 16.5 %convolution_convert_fusion = bf16[2048,576]{0,1:T(8,128)(2,1)S(1)} fusion(bf16[2048,4608]{1,0:T(8,128)(2,1)} %all-gather.2.cloned.1.call-done, bf16[4608,576]{0,1:T(8,128)(2,1)} %param.8), kind=kOutput, calls=%fused_computation.10 | convolution fusion | flops 10872815616 | bytes 26542080 | tf_op jit(solution)/shard_map/dot_general | solution.py:32
  389.6 1.6 copy.21
  391.2 0.0 all-reduce.2.cloned.1.call-update
  391.2 55.0 %all-reduce.2.cloned.1.call-done = bf16[8,256,576]{1,2,0:T(8,128)(2,1)} async-done(((bf16[8,256,576]{1,2,0:T(8,128)(2,1)}), bf16[8,256,576]{1,2,0:T(8,128)(2,1)}) %all-reduce.2.cloned.1.call-update) | async-done | bytes 2359312 | tf_op jit(solution)/shard_map/psum | solution.py:37
  446.1 6.1 %all-to-all-start = ((bf16[8,256,576]{1,2,0:T(8,128)(2,1)}), bf16[8,256,576]{1,2,0:T(8,128)(2,1)S(1)}, u32[]{:S(2)}, u32[]{:S(2)}) async-start(bf16[8,256,576]{1,2,0:T(8,128)(2,1)} %all-reduce.2.cloned.1.call-done), calls=%async_computation | async-start | bytes 4718592 | tf_op jit(solution)/shard_map/all_to_all | solution.py:38
  452.2 4.3 copy.14
  457.1 46.4 %all-to-all-done = bf16[8,256,576]{1,2,0:T(8,128)(2,1)S(1)} async-done(((bf16[8,256,576]{1,2,0:T(8,128)(2,1)}), bf16[8,256,576]{1,2,0:T(8,128)(2,1)S(1)}, u32[]{:S(2)}, u32[]{:S(2)}) %all-to-all-start) | async-done | bytes 2359328 | tf_op jit(solution)/shard_map/all_to_all | solution.py:38
  503.5 1.2 abs_reduce_fusion.2
  504.7 3.3 multiply_reduce_fusion
  508.0 0.0 copy-done.3
  508.0 0.0 copy-start.4
  508.1 4.8 abs_reduce_fusion.1
  512.8 2.2 pad_maximum_fusion.1
  515.0 0.1 slice_reduce_fusion
  515.1 41.9 %pmax.7 = f32[3]{0:T(128)S(1)} all-reduce(f32[3]{0:T(128)S(1)} %pad_maximum_fusion.1), channel_id=1, replica_groups=mesh['dp'=8,'tensor'=4] {'dp','tensor'}, use_global_device_ids=true, to_apply=%region_6.7 | all-reduce | flops 3 | bytes 24 | tf_op jit(solution)/shard_map/pmax | solution.py:42
  557.0 0.1 copy.16
  557.1 0.5 maximum_divide_fusion
  557.6 4.3 copy.17
  561.9 2.4 copy.18
  564.3 0.7 pad_maximum_fusion
  (12 shorter events, 0.0 us)
Async XLA Ops:
  7.2 365.9 %all-gather.2.cloned.1.call-start = ((), (), s32[]{:S(2)}) async-start(), calls=%async_computation.1 | async-start | bytes 21233664 | tf_op jit(solution)/shard_map/all_gather | solution.py:33
  7.9 438.2 %all-reduce.2.cloned.1.call-start = ((), (), s32[]{:S(2)}) async-start(), calls=%async_computation.2 | async-start | bytes 4718592 | tf_op jit(solution)/shard_map/psum | solution.py:37
  446.1 57.4 %all-to-all-start = ((bf16[8,256,576]{1,2,0:T(8,128)(2,1)}), bf16[8,256,576]{1,2,0:T(8,128)(2,1)S(1)}, u32[]{:S(2)}, u32[]{:S(2)}) async-start(bf16[8,256,576]{1,2,0:T(8,128)(2,1)} %all-reduce.2.cloned.1.call-done), calls=%async_computation | async-start | bytes 4718592 | tf_op jit(solution)/shard_map/all_to_all | solution.py:38
  452.2 52.5 %copy-start.2 = (f32[4608]{0:T(1024)S(1)}, f32[4608]{0:T(1024)}, u32[]{:S(2)}) copy-start(f32[4608]{0:T(1024)} %param.10) | copy-start | bytes 55300
  456.5 51.5 %copy-start.3 = (f32[4608]{0:T(1024)S(1)}, f32[4608]{0:T(1024)}, u32[]{:S(2)}) copy-start(f32[4608]{0:T(1024)} %param.11) | copy-start | bytes 55300
  503.5 4.5 copy-start
  508.0 7.0 %copy-start.4 = (f32[3,1024]{1,0:T(4,128)S(1)}, f32[3,1024]{1,0:T(4,128)}, u32[]{:S(2)}) copy-start(f32[3,1024]{1,0:T(4,128)} %param.13) | copy-start | bytes 36868
  512.8 49.0 %copy-start.1 = (bf16[256,4608]{0,1:T(8,128)(2,1)S(1)}, bf16[256,4608]{0,1:T(8,128)(2,1)}, u32[]{:S(2)}) copy-start(bf16[256,4608]{0,1:T(8,128)(2,1)} %get-tuple-element.15) | copy-start | bytes 7077892
  557.0 7.3 %copy-start.5 = (f32[3]{0:T(128)}, f32[3]{0:T(128)S(1)}, u32[]{:S(2)}) copy-start(f32[3]{0:T(128)S(1)} %pmax.7) | copy-start | bytes 40
Sparse Core Ops, SparseCore 0:
  9.5 363.4 all-gather.1
  391.3 54.8 all-reduce.1
where the time goes:
time: 572 us
  waiting for transfers between devices  467 us (82%)
  blocking collectives  41.9 us (7%)
  matrix products  16.5 us (3%)
  between operations  14.7 us (3%)
  other arithmetic  12.8 us (2%)
  local copies, waits for them, and re-layouts  12.6 us (2%)
  starting transfers between devices  6.13 us (1%)
    all_gather x1, waiting for transfers between devices, on_device(): lax.all_gather(hidden, 'dp', axis=0, tiled=True)  365 us
    psum x1, waiting for transfers between devices, on_device(): lax.psum(partial_value.astype(jnp.bfloat16), 'tensor').astype(jnp.float32)  55 us
    all_to_all x1, waiting for transfers between devices, on_device(): lax.all_to_all(column_total.astype(jnp.bfloat16), 'dp', split_axis=0, con...  46.4 us
    pmax x1, blocking collectives, on_device(): peak_values = lax.pmax(peak_values, ('dp', 'tensor'))  41.9 us
    dot_general x1, matrix products, on_device(): jnp.dot(lax.all_gather(hidden, 'dp', axis=0, tiled=True), down_weight, pr...  16.5 us
  transfers between devices with their start and end apart: 3, of which 3 were waited for; matrix products, arithmetic and copies ran while one was open for 1% of the time, Pallas kernels for 0%

commit v1 on v0

v1 whole, which is shorter than its diff:
```python
import functools

import jax
import jax.numpy as jnp
from jax import lax
from jax.experimental import pallas as pl
from jax.experimental.pallas import tpu as pltpu
from jax.sharding import PartitionSpec as P

norm_epsilon = 1e-06
float_limit = 448.0
LANES = 128
ROW_STEP = 16
ANY = pl.ANY
VMEM_LIMIT = 60 * 1024 * 1024


def rms_norm(values, gain_vector):
    return (
        values
        * lax.rsqrt(jnp.mean(values * values, axis=-1, keepdims=True) + norm_epsilon)
        * gain_vector
    )


def finish(summed, stream_in, post_gain, pre_gain, stale_scale):
    stream = stream_in.astype(jnp.float32) + rms_norm(summed, post_gain)
    normed = rms_norm(stream, pre_gain)
    cast_rows = (jnp.clip(normed * stale_scale, -float_limit, float_limit) / stale_scale).astype(
        jnp.bfloat16
    )
    peak_values = jnp.stack(
        [jnp.max(jnp.abs(summed)), jnp.max(jnp.abs(stream)), jnp.max(jnp.abs(normed))]
    )
    return (cast_rows, stream.astype(jnp.bfloat16), peak_values)


def histories(peak_values, amax_history):
    new_history = jnp.concatenate([peak_values[:, None], amax_history[:, :-1]], axis=1)
    new_scales = float_limit / jnp.maximum(jnp.max(new_history, axis=1), 1.0)
    return new_history, new_scales


def general(hidden, down_weight, residual, post_gain, pre_gain, cast_scale, amax_history):
    partial_value = jnp.dot(
        lax.all_gather(hidden, "dp", axis=0, tiled=True),
        down_weight,
        preferred_element_type=jnp.float32,
    )
    column_total = lax.psum(partial_value.astype(jnp.bfloat16), "tensor")
    summed = lax.all_to_all(
        column_total, "dp", split_axis=0, concat_axis=1, tiled=True
    ).astype(jnp.float32)
    cast_out, residual_out, peak_values = finish(
        summed, residual, post_gain, pre_gain, cast_scale[0]
    )
    peak_values = lax.pmax(peak_values, ("dp", "tensor"))
    new_history, new_scales = histories(peak_values, amax_history)
    return (cast_out, residual_out, peak_values, new_history, new_scales)


def matmul_kernel(n, nt, where_ref, *refs):
    own_w, other_w, own_h = refs[:3]
    ups, downs = refs[3 : 2 + n], refs[2 + n : 1 + 2 * n]
    out, w_buf, h_buf, o_buf, w_sem, h_sem, o_sem = refs[1 + 2 * n :]
    line, pair, member = where_ref[0], where_ref[1], where_ref[2]
    half = own_w.shape[0]
    rows = own_h.shape[0]
    piece = rows // nt

    def w_copy(src, place, k):
        return pltpu.make_async_copy(
            src, w_buf.at[pl.ds(pl.multiple_of(place * half, half), half)], w_sem.at[k]
        )

    def h_copy(src, r):
        return pltpu.make_async_copy(src, h_buf.at[r % 2], h_sem.at[r % 2])

    def fetch(r):
        @pl.when(line == r)
        def _():
            h_copy(own_h, r).start()

        for s in range(1, n):

            @pl.when(line + s == r)
            def _():
                h_copy(ups[s - 1], r).start()

            @pl.when(line - s == r)
            def _():
                h_copy(downs[s - 1], r).start()

    def o_copies(r):
        found = []
        for k in range(nt):
            place = pl.multiple_of((member ^ k) * piece, piece)
            found.append(
                pltpu.make_async_copy(
                    o_buf.at[r % 2, pl.ds(place, piece)], out.at[k, r], o_sem.at[r % 2, k]
                )
            )
        return found

    w_copy(own_w, pair, 0).start()
    w_copy(other_w, 1 - pair, 1).start()
    fetch(0)
    w_copy(own_w, pair, 0).wait()
    w_copy(other_w, 1 - pair, 1).wait()
    for r in range(n):
        if r + 1 < n:
            fetch(r + 1)
        h_copy(own_h, r).wait()
        if r >= 2:
            for copy in o_copies(r - 2):
                copy.wait()
        o_buf[r % 2] = lax.dot_general(
            h_buf[r % 2],
            w_buf[...],
            (((1,), (1,)), ((), ())),
            preferred_element_type=jnp.float32,
        ).astype(jnp.bfloat16)
        for copy in o_copies(r):
            copy.start()
    for r in range(max(n - 2, 0), n):
        for copy in o_copies(r):
            copy.wait()


def multiply(where, own_w, other_w, own_h, ups, downs, n, nt):
    rows, depth = own_h.shape
    columns = 2 * own_w.shape[0]
    return pl.pallas_call(
        functools.partial(matmul_kernel, n, nt),
        out_shape=jax.ShapeDtypeStruct((nt, n, rows // nt, columns), jnp.bfloat16),
        in_specs=[pl.BlockSpec(memory_space=pltpu.SMEM)]
        + [pl.BlockSpec(memory_space=ANY)] * (3 + 2 * (n - 1)),
        out_specs=pl.BlockSpec(memory_space=ANY),
        scratch_shapes=[
            pltpu.VMEM((columns, depth), jnp.bfloat16),
            pltpu.VMEM((2, rows, depth), jnp.bfloat16),
            pltpu.VMEM((2, rows, columns), jnp.bfloat16),
            pltpu.SemaphoreType.DMA((2,)),
            pltpu.SemaphoreType.DMA((2,)),
            pltpu.SemaphoreType.DMA((2, nt)),
        ],
        compiler_params=pltpu.CompilerParams(vmem_limit_bytes=VMEM_LIMIT),
        cost_estimate=pl.CostEstimate(
            flops=2 * n * rows * depth * columns,
            bytes_accessed=2 * (n * rows + columns) * depth,
            transcendentals=0,
        ),
        name="multiply",
    )(where, own_w, other_w, own_h, *ups, *downs)


def norm_kernel(n, nt, where_ref, scale_ref, residual, post_ref, pre_ref, *refs):
    pieces = refs[:nt]
    cast_out, stream_out, peaks_ref = refs[nt : nt + 3]
    q_buf, r_buf, c_buf, s_buf, t_buf, in_sem, r_sem, c_sem, s_sem = refs[nt + 3 :]
    line, member = where_ref[0], where_ref[2]
    piece, block = q_buf.shape[2], q_buf.shape[3]
    width = n * block
    scale = scale_ref[0]
    slices = [pl.ds(j * LANES, LANES) for j in range(block // LANES)]

    def row_place(k):
        return pl.ds(pl.multiple_of((member ^ k) * piece, piece), piece)

    def in_copy(k):
        return pltpu.make_async_copy(pieces[k], q_buf.at[k % 2], in_sem.at[k % 2])

    def column(i):
        return lax.rem(line - i + n, n)

    def res_copy(k, i):
        place = pl.ds(pl.multiple_of(column(i) * block, block), block)
        return pltpu.make_async_copy(
            residual.at[row_place(k), place], r_buf.at[k % 2, i], r_sem.at[k % 2, i]
        )

    def out_copies(k, i):
        place = pl.ds(pl.multiple_of(column(i) * block, block), block)
        return (
            pltpu.make_async_copy(
                c_buf.at[k % 2, i], cast_out.at[row_place(k), place], c_sem.at[k % 2, i]
            ),
            pltpu.make_async_copy(
                s_buf.at[k % 2, i], stream_out.at[row_place(k), place], s_sem.at[k % 2, i]
            ),
        )

    def start_in(k):
        in_copy(k).start()
        for i in range(n):
            res_copy(k, i).start()

    zero = jnp.zeros((ROW_STEP, LANES), jnp.float32)
    tops = (zero, zero, zero)
    start_in(0)
    for k in range(nt):
        if k + 1 < nt:
            start_in(k + 1)
        in_copy(k).wait()
        for i in range(n):
            res_copy(k, i).wait()
        if k >= 2:
            for i in range(n):
                for copy in out_copies(k - 2, i):
                    copy.wait()
        slot = k % 2

        def step(index, carry, slot=slot):
            top_a, top_b, top_c = carry
            here = pl.ds(pl.multiple_of(index * ROW_STEP, ROW_STEP), ROW_STEP)
            total = zero
            for i in range(n):
                for lanes in slices:
                    v = q_buf[slot, i, here, lanes].astype(jnp.float32)
                    total = total + v * v
                    top_a = jnp.maximum(top_a, jnp.abs(v))
            inverse = lax.rsqrt(jnp.sum(total, axis=-1, keepdims=True) / width + norm_epsilon)
            total = zero
            for i in range(n):
                for lanes in slices:
                    v = q_buf[slot, i, here, lanes].astype(jnp.float32)
                    gain = post_ref[column(i), :, lanes]
                    v = r_buf[slot, i, here, lanes].astype(jnp.float32) + v * inverse * gain
                    t_buf[i, :, lanes] = v
                    s_buf[slot, i, here, lanes] = v.astype(jnp.bfloat16)
                    total = total + v * v
                    top_b = jnp.maximum(top_b, jnp.abs(v))
            inverse = lax.rsqrt(jnp.sum(total, axis=-1, keepdims=True) / width + norm_epsilon)
            for i in range(n):
                for lanes in slices:
                    gain = pre_ref[column(i), :, lanes]
                    v = t_buf[i, :, lanes] * inverse * gain
                    top_c = jnp.maximum(top_c, jnp.abs(v))
                    v = jnp.clip(v * scale, -float_limit, float_limit) / scale
                    c_buf[slot, i, here, lanes] = v.astype(jnp.bfloat16)
            return top_a, top_b, top_c

        tops = lax.fori_loop(0, piece // ROW_STEP, step, tops)
        for i in range(n):
            for copy in out_copies(k, i):
                copy.start()
    for a in range(3):
        peaks_ref[a] = jnp.broadcast_to(jnp.max(tops[a]), peaks_ref.shape[1:])
    for k in range(max(nt - 2, 0), nt):
        for i in range(n):
            for copy in out_copies(k, i):
                copy.wait()


def normalise(where, scale, residual, post_gain, pre_gain, pieces, n, nt):
    rows, width = residual.shape
    block, piece = width // n, rows // nt
    return pl.pallas_call(
        functools.partial(norm_kernel, n, nt),
        out_shape=(
            jax.ShapeDtypeStruct((rows, width), jnp.bfloat16),
            jax.ShapeDtypeStruct((rows, width), jnp.bfloat16),
            jax.ShapeDtypeStruct((3, 8, LANES), jnp.float32),
        ),
        in_specs=[pl.BlockSpec(memory_space=pltpu.SMEM)] * 2
        + [pl.BlockSpec(memory_space=ANY)]
        + [pl.BlockSpec(memory_space=pltpu.VMEM)] * 2
        + [pl.BlockSpec(memory_space=ANY)] * nt,
        out_specs=(
            pl.BlockSpec(memory_space=ANY),
            pl.BlockSpec(memory_space=ANY),
            pl.BlockSpec(memory_space=pltpu.VMEM),
        ),
        scratch_shapes=[
            pltpu.VMEM((2, n, piece, block), jnp.bfloat16),
            pltpu.VMEM((2, n, piece, block), jnp.bfloat16),
            pltpu.VMEM((2, n, piece, block), jnp.bfloat16),
            pltpu.VMEM((2, n, piece, block), jnp.bfloat16),
            pltpu.VMEM((n, ROW_STEP, block), jnp.float32),
            pltpu.SemaphoreType.DMA((2,)),
            pltpu.SemaphoreType.DMA((2, n)),
            pltpu.SemaphoreType.DMA((2, n)),
            pltpu.SemaphoreType.DMA((2, n)),
        ],
        compiler_params=pltpu.CompilerParams(vmem_limit_bytes=VMEM_LIMIT),
        cost_estimate=pl.CostEstimate(
            flops=30 * rows * width, bytes_accessed=8 * rows * width, transcendentals=0
        ),
        name="normalise",
    )(
        where,
        scale,
        residual,
        post_gain.reshape(n, 1, block),
        pre_gain.reshape(n, 1, block),
        *pieces,
    )


def tiled(n, nt, hidden, down_weight, residual, post_gain, pre_gain, cast_scale, amax_history):
    f32, bf16 = jnp.float32, jnp.bfloat16
    place = lax.axis_index("dp")
    member = lax.axis_index("tensor")
    line, pair = place // 2, place % 2
    where = jnp.stack([line, pair, member]).astype(jnp.int32)

    def along(value, step, first, last):
        hops = [
            (z * 2 + p, (z + step) * 2 + p) for z in range(first, last) for p in range(2)
        ]
        return lax.ppermute(value, "dp", hops)

    def over_tensor(value, k):
        return lax.ppermute(value, "tensor", [(t, t ^ k) for t in range(nt)])

    own_w = down_weight.T
    other_w = lax.ppermute(own_w, "dp", [(d, d ^ 1) for d in range(2 * n)])
    halves = 2
    cut = hidden.shape[0] // halves
    parts = [hidden[i * cut : (i + 1) * cut] for i in range(halves)]
    ups, downs = [], []
    up_parts, down_parts = list(parts), list(parts)
    for s in range(1, n):
        up_parts = [along(v, -1, 1, n - s + 1) for v in up_parts]
        down_parts = [along(v, 1, s - 1, n - 1) for v in down_parts]
        ups.append(jnp.concatenate(up_parts, axis=0))
        downs.append(jnp.concatenate(down_parts, axis=0))

    partial = multiply(where, own_w, other_w, hidden, ups, downs, n, nt)

    near = over_tensor(jnp.concatenate([partial[k : k + 1] for k in range(1, nt, 2)]), 1)
    totals = partial[0].astype(f32) + near[0].astype(f32)
    for k in range(2, nt, 2):
        pair_sum = (partial[k].astype(f32) + near[k // 2].astype(f32)).astype(bf16)
        totals = totals + over_tensor(pair_sum, k).astype(f32)
    totals = totals.astype(bf16)

    blocks = []
    for k in range(n):
        mine = lax.dynamic_index_in_dim(totals, lax.rem(line + k, n), 0, keepdims=True)
        if k:
            hops = [(z * 2 + p, (z + k) % n * 2 + p) for z in range(n) for p in range(2)]
            mine = lax.ppermute(mine, "dp", hops)
        blocks.append(mine)
    own_rows = jnp.concatenate(blocks, axis=0)

    pieces = [None] * nt
    pieces[0] = own_rows
    for k in range(2, nt, 2):
        pieces[k] = over_tensor(own_rows, k)
    for k in range(1, nt, 2):
        pieces[k] = over_tensor(pieces[k - 1], 1)

    cast_out, residual_out, peaks = normalise(
        where, cast_scale, residual, post_gain, pre_gain, pieces, n, nt
    )
    peaks = peaks[:, 0, 0]
    bit = 1
    while bit < 2 * n:
        peaks = jnp.maximum(
            peaks, lax.ppermute(peaks, "dp", [(d, d ^ bit) for d in range(2 * n)])
        )
        bit *= 2
    new_history, new_scales = histories(peaks, amax_history)
    return (cast_out, residual_out, peaks, new_history, new_scales)


def power_of_two(value):
    return value & (value - 1) == 0


def solution(mesh):
    ndp, nt = mesh.shape["dp"], mesh.shape["tensor"]

    def on_device(hidden, down_weight, residual, *rest):
        rows, half = hidden.shape[0], down_weight.shape[1]
        fits = (
            ndp >= 4
            and power_of_two(ndp)
            and nt >= 2
            and power_of_two(nt)
            and 2 * half % LANES == 0
            and half % ROW_STEP == 0
            and rows % (nt * ROW_STEP) == 0
            and hidden.shape[1] % LANES == 0
        )
        if fits:
            return tiled(ndp // 2, nt, hidden, down_weight, residual, *rest)
        return general(hidden, down_weight, residual, *rest)

    in_specs = (P("dp", "tensor"), P("tensor", "dp"), P("dp", None), P(), P(), P(), P())
    out_specs = (P("dp", None), P("dp", None), P(), P(), P())
    return jax.shard_map(
        on_device, mesh=mesh, in_specs=in_specs, out_specs=out_specs, check_vma=False
    )
```

time: 572 us -> 272 us (0.48)
  waiting for transfers between devices: 467 us -> 170 us
  blocking collectives: 41.9 us -> 0 us
  starting transfers between devices: 6.13 us -> 42.9 us
  Pallas kernels: 0 us -> 31.5 us
  matrix products: 16.5 us -> 0 us
  between operations: 14.7 us -> 1.58 us
    all_gather x1 -> x0, waiting for transfers between devices: 365 us -> none  [on_device(): lax.all_gather(hidden, 'dp', axis=0, tiled=True)]
    ppermute x0 -> x24, waiting for transfers between devices: none -> 170 us  [the longest x12 116 us: along(): return lax.ppermute(value, 'dp', hops)]
    psum x1 -> x0, waiting for transfers between devices: 55 us -> none  [on_device(): lax.psum(partial_value.astype(jnp.bfloat16), 'tensor').astype(jnp.float32)]
    all_to_all x1 -> x0, waiting for transfers between devices: 46.4 us -> none  [on_device(): lax.all_to_all(column_total.astype(jnp.bfloat16), 'dp', split_axis=0, con...]
    ppermute x0 -> x24, starting transfers between devices: none -> 42.9 us  [the longest x12 29.9 us: along(): return lax.ppermute(value, 'dp', hops)]
    pmax x1 -> x0, blocking collectives: 41.9 us -> none  [on_device(): peak_values = lax.pmax(peak_values, ('dp', 'tensor'))]
    pallas_call x0 -> x2, Pallas kernels: none -> 31.5 us  [the longest x1 21.7 us: multiply(): pl.pallas_call(functools.partial(matmul_kernel, n, nt), out_shape=jax.Sha...]
    dot_general x1 -> x0, matrix products: 16.5 us -> none  [on_device(): jnp.dot(lax.all_gather(hidden, 'dp', axis=0, tiled=True), down_weight, pr...]
  transfers between devices with their start and end apart: 3 -> 24, of which waited for: 3 -> 15; matrix products, arithmetic and copies ran while one was open for 1% -> 6% of each run, Pallas kernels for 0% -> 0%
where the time goes in v1:
time: 272 us; the launch traced here: 270 us
  waiting for transfers between devices  170 us (62%)
  starting transfers between devices  42.9 us (16%)
  Pallas kernels  31.5 us (12%)
  other arithmetic  15.1 us (6%)
  local copies, waits for them, and re-layouts  8.6 us (3%)
    ppermute x12, waiting for transfers between devices, along(): return lax.ppermute(value, 'dp', hops)  116 us
    ppermute x5, waiting for transfers between devices, over_tensor(): return lax.ppermute(value, 'tensor', [(t, t ^ k) for t in range(nt)])  32.7 us
    ppermute x12, starting transfers between devices, along(): return lax.ppermute(value, 'dp', hops)  29.9 us
    pallas_call x1, Pallas kernels, multiply(): pl.pallas_call(functools.partial(matmul_kernel, n, nt), out_shape=jax.Sha...  21.7 us
    ppermute x3, waiting for transfers between devices, tiled(): lax.ppermute(peaks, 'dp', [(d, d ^ bit) for d in range(2 * n)])  11.1 us
    ppermute x3, waiting for transfers between devices, tiled(): mine = lax.ppermute(mine, 'dp', hops)  10.7 us
    pallas_call x1, Pallas kernels, normalise(): pl.pallas_call(functools.partial(norm_kernel, n, nt), out_shape=(jax.Shap...  9.81 us
    ppermute x3, starting transfers between devices, tiled(): mine = lax.ppermute(mine, 'dp', hops)  9.64 us
  transfers between devices with their start and end apart: 24, of which 15 were waited for; matrix products, arithmetic and copies ran while one was open for 6% of the time, Pallas kernels for 0%

profile of v1, /device:TPU:10, one launch (start us, length us, event | category | flops | bytes accessed | tf_op | source)
XLA Modules:
  0.0 269.9 jit_solution(14849442862127075919)
XLA Ops:
  2.2 3.2 %fusion.3 = (bf16[128,4608]{1,0:T(8,128)(2,1)}, bf16[128,4608]{1,0:T(8,128)(2,1)}) fusion(bf16[256,4608]{1,0:T(8,128)(2,1)} %refs_2_.1), kind=kLoop, calls=%fused_computation.22 | loop fusion | bytes 4718592 | tf_op jit(solution)/shard_map/slice | solution.py:320
  9.7 3.9 %collective-permute-start.7 = (bf16[128,4608]{1,0:T(8,128)(2,1)}, bf16[128,4608]{1,0:T(8,128)(2,1)S(1)}, u32[]{:S(2)}, u32[]{:S(2)}) collective-permute-start(bf16[128,4608]{1,0:T(8,128)(2,1)} %get-tuple-element.15), channel_id=1, source_target_pairs={{0,8},{4,12},{8,16},{12,20},{16,24},{20,28},{1,9},{5,13},{9,17},{1... | collective-permute-start | bytes 3538952 | tf_op jit(solution)/shard_map/ppermute | solution.py:311
  13.6 3.6 %collective-permute-start.8 = (bf16[128,4608]{1,0:T(8,128)(2,1)}, bf16[128,4608]{1,0:T(8,128)(2,1)S(1)}, u32[]{:S(2)}, u32[]{:S(2)}) collective-permute-start(bf16[128,4608]{1,0:T(8,128)(2,1)} %get-tuple-element.16), channel_id=1, source_target_pairs={{0,8},{4,12},{8,16},{12,20},{16,24},{20,28},{1,9},{5,13},{9,17},{1... | collective-permute-start | bytes 3538952 | tf_op jit(solution)/shard_map/ppermute | solution.py:311
  17.9 18.6 %collective-permute-done.1 = bf16[128,4608]{1,0:T(8,128)(2,1)} collective-permute-done((bf16[128,4608]{1,0:T(8,128)(2,1)}, bf16[128,4608]{1,0:T(8,128)(2,1)}, u32[]{:S(2)}, u32[]{:S(2)}) %collective-permute-start.1) | collective-permute-done | bytes 1179680 | tf_op jit(solution)/shard_map/ppermute | solution.py:311
  38.8 22.8 %collective-permute-done.2 = bf16[128,4608]{1,0:T(8,128)(2,1)S(1)} collective-permute-done((bf16[128,4608]{1,0:T(8,128)(2,1)}, bf16[128,4608]{1,0:T(8,128)(2,1)S(1)}, u32[]{:S(2)}, u32[]{:S(2)}) %collective-permute-start.2) | collective-permute-done | bytes 1179680 | tf_op jit(solution)/shard_map/ppermute | solution.py:311
  64.0 3.6 %collective-permute-start.9 = (bf16[128,4608]{1,0:T(8,128)(2,1)S(1)}, bf16[128,4608]{1,0:T(8,128)(2,1)S(1)}, u32[]{:S(2)}, u32[]{:S(2)}) collective-permute-start(bf16[128,4608]{1,0:T(8,128)(2,1)S(1)} %collective-permute-done.7), channel_id=1, source_target_pairs={{8,16},{12,20},{16,24},{20,28},{9,17},{13,21},{17,25},{21,29},{10,... | collective-permute-start | bytes 3538952 | tf_op jit(solution)/shard_map/ppermute | solution.py:311
  69.5 2.8 %pad_maximum_fusion.refs_3_ = bf16[256,4608]{1,0:T(8,128)(2,1)} fusion(bf16[128,4608]{1,0:T(8,128)(2,1)S(1)} %collective-permute-done.2, bf16[128,4608]{1,0:T(8,128)(2,1)} %collective-permute-done.1), kind=kLoop, calls=%fused_computation | loop fusion | flops 4718592 | bytes 4718592 | tf_op jit(solution)/shard_map/concatenate | solution.py:326
  73.9 13.0 %collective-permute-done.3 = bf16[128,4608]{1,0:T(8,128)(2,1)S(1)} collective-permute-done((bf16[128,4608]{1,0:T(8,128)(2,1)}, bf16[128,4608]{1,0:T(8,128)(2,1)S(1)}, u32[]{:S(2)}, u32[]{:S(2)}) %collective-permute-start.3) | collective-permute-done | bytes 1179680 | tf_op jit(solution)/shard_map/ppermute | solution.py:311
  86.9 2.4 collective-permute-start.5
  89.3 21.4 %collective-permute-done.4 = bf16[128,4608]{1,0:T(8,128)(2,1)S(1)} collective-permute-done((bf16[128,4608]{1,0:T(8,128)(2,1)S(1)}, bf16[128,4608]{1,0:T(8,128)(2,1)S(1)}, u32[]{:S(2)}, u32[]{:S(2)}) %collective-permute-start.4) | collective-permute-done | bytes 1179680 | tf_op jit(solution)/shard_map/ppermute | solution.py:311
  110.8 3.8 %collective-permute-start.6 = (bf16[128,4608]{1,0:T(8,128)(2,1)S(1)}, bf16[128,4608]{1,0:T(8,128)(2,1)S(1)}, u32[]{:S(2)}, u32[]{:S(2)}) collective-permute-start(bf16[128,4608]{1,0:T(8,128)(2,1)S(1)} %collective-permute-done.4), channel_id=1, source_target_pairs={{8,0},{12,4},{9,1},{13,5},{10,2},{14,6},{11,3},{15,7}} | collective-permute-start | bytes 3538952 | tf_op jit(solution)/shard_map/ppermute | solution.py:311
  119.4 16.0 %collective-permute-done.5 = bf16[128,4608]{1,0:T(8,128)(2,1)S(1)} collective-permute-done((bf16[128,4608]{1,0:T(8,128)(2,1)S(1)}, bf16[128,4608]{1,0:T(8,128)(2,1)S(1)}, u32[]{:S(2)}, u32[]{:S(2)}) %collective-permute-start.5) | collective-permute-done | bytes 1179680 | tf_op jit(solution)/shard_map/ppermute | solution.py:311
  135.4 23.9 %collective-permute-done.6 = bf16[128,4608]{1,0:T(8,128)(2,1)S(1)} collective-permute-done((bf16[128,4608]{1,0:T(8,128)(2,1)S(1)}, bf16[128,4608]{1,0:T(8,128)(2,1)S(1)}, u32[]{:S(2)}, u32[]{:S(2)}) %collective-permute-start.6) | collective-permute-done | bytes 1179680 | tf_op jit(solution)/shard_map/ppermute | solution.py:311
  162.5 21.7 %multiply.1 = bf16[4,4,64,1152]{3,2,1,0:T(8,128)(2,1)} custom-call(s32[3]{0:T(128)} %pad_add_fusion.where_ref, bf16[576,4608]{1,0:T(8,128)(2,1)} %bitcast.13, bf16[576,4608]{1,0:T(8,128)(2,1)} %collective-permute-done.refs_1_, bf16[256,4608]{1,0:T(8,128)(2,1)} %refs_2_.1, bf16[256,4608]{1,0:T(8,128)(2,1)} %pad_maximum_fusion.refs_3_, ...), custom_call_target="tpu_custom_call" | custom-call | flops 10871635968 | bytes 20054016 | tf_op jit(solution)/shard_map/multiply/pallas_call | solution.py:133
  185.9 2.8 %collective-permute-done.13 = bf16[2,4,64,1152]{3,2,1,0:T(8,128)(2,1)S(1)} collective-permute-done((bf16[2,4,64,1152]{3,2,1,0:T(8,128)(2,1)S(1)}, bf16[2,4,64,1152]{3,2,1,0:T(8,128)(2,1)S(1)}, u32[]{:S(2)}, u32[]{:S(2)}) %collective-permute-start.13) | collective-permute-done | bytes 1179680 | tf_op jit(solution)/shard_map/ppermute | solution.py:314
  190.2 15.1 %collective-permute-done.14 = bf16[4,64,1152]{2,1,0:T(8,128)(2,1)} collective-permute-done((bf16[4,64,1152]{2,1,0:T(8,128)(2,1)}, bf16[4,64,1152]{2,1,0:T(8,128)(2,1)}, u32[]{:S(2)}, u32[]{:S(2)}) %collective-permute-start.14) | collective-permute-done | bytes 589856 | tf_op jit(solution)/shard_map/ppermute | solution.py:314
  206.7 5.7 %collective-permute-start.15 = (bf16[1,64,1152]{2,1,0:T(8,128)(2,1)S(1)}, bf16[1,64,1152]{2,1,0:T(8,128)(2,1)S(1)}, u32[]{:S(2)}, u32[]{:S(2)}) collective-permute-start(bf16[1,64,1152]{2,1,0:T(8,128)(2,1)S(1)} %get-tuple-element.20), channel_id=1, source_target_pairs={{0,8},{4,12},{8,16},{12,20},{16,24},{20,28},{24,0},{28,4},{1,9},{5... | collective-permute-start | bytes 442376 | tf_op jit(solution)/shard_map/ppermute | solution.py:343
  216.4 6.2 %collective-permute-done.15 = bf16[1,64,1152]{2,1,0:T(8,128)(2,1)S(1)} collective-permute-done((bf16[1,64,1152]{2,1,0:T(8,128)(2,1)S(1)}, bf16[1,64,1152]{2,1,0:T(8,128)(2,1)S(1)}, u32[]{:S(2)}, u32[]{:S(2)}) %collective-permute-start.15) | collective-permute-done | bytes 147488 | tf_op jit(solution)/shard_map/ppermute | solution.py:343
  224.6 2.6 collective-permute-done.17
  227.8 14.7 %collective-permute-done.19.refs_2_ = bf16[4,64,1152]{2,1,0:T(8,128)(2,1)S(1)} collective-permute-done((bf16[4,64,1152]{2,1,0:T(8,128)(2,1)S(1)}, bf16[4,64,1152]{2,1,0:T(8,128)(2,1)S(1)}, u32[]{:S(2)}, u32[]{:S(2)}) %collective-permute-start.19) | collective-permute-done | bytes 589856 | tf_op jit(solution)/shard_map/ppermute | solution.py:314
  246.3 9.8 %normalise.1 = (bf16[256,4608]{1,0:T(8,128)(2,1)}, bf16[256,4608]{1,0:T(8,128)(2,1)}, f32[3,8,128]{2,1,0:T(8,128)}) custom-call(s32[3]{0:T(128)} %pad_add_fusion.where_ref, f32[1]{0:T(128)S(6)} %copy.14.scale_ref, bf16[256,4608]{1,0:T(8,128)(2,1)} %residual.1, f32[4,1,1152]{2,1,0:T(1,128)} %reshape.25.post_ref, f32[4,1,1152]{2,1,0:T(1,128)} %reshape.26.pre_ref, ...), custom_call_target="tpu_custom_call" | custom-call | flops 35389440 | bytes 9437184 | tf_op jit(solution)/shard_map/normalise/pallas_call | solution.py:258
  257.5 3.1 %collective-permute-done.21 = f32[3]{0:T(128)S(1)} collective-permute-done((f32[3]{0:T(128)S(1)}, f32[3]{0:T(128)S(1)}, u32[]{:S(2)}, u32[]{:S(2)}) %collective-permute-start.21) | collective-permute-done | bytes 44 | tf_op jit(solution)/shard_map/ppermute | solution.py:361
  260.5 3.6 %collective-permute-done.22 = f32[3]{0:T(128)S(1)} collective-permute-done((f32[3]{0:T(128)S(1)}, f32[3]{0:T(128)S(1)}, u32[]{:S(2)}, u32[]{:S(2)}) %collective-permute-start.22) | collective-permute-done | bytes 44 | tf_op jit(solution)/shard_map/ppermute | solution.py:361
  264.1 4.5 %collective-permute-done.23 = f32[3]{0:T(128)S(1)} collective-permute-done((f32[3]{0:T(128)S(1)}, f32[3]{0:T(128)S(1)}, u32[]{:S(2)}, u32[]{:S(2)}) %collective-permute-start.23) | collective-permute-done | bytes 44 | tf_op jit(solution)/shard_map/ppermute | solution.py:361
  (67 shorter events, 39.5 us)
Async XLA Ops:
  0.6 161.8 %collective-permute-start = (bf16[576,4608]{1,0:T(8,128)(2,1)}, bf16[576,4608]{1,0:T(8,128)(2,1)}, u32[]{:S(2)}, u32[]{:S(2)}) collective-permute-start(bf16[576,4608]{1,0:T(8,128)(2,1)} %bitcast.12), channel_id=1, source_target_pairs={{0,4},{4,0},{8,12},{12,8},{16,20},{20,16},{24,28},{28,24},{1,5},{5... | collective-permute-start | bytes 15925256 | tf_op jit(solution)/shard_map/ppermute | solution.py:317
  5.4 31.0 %collective-permute-start.1 = (bf16[128,4608]{1,0:T(8,128)(2,1)}, bf16[128,4608]{1,0:T(8,128)(2,1)}, u32[]{:S(2)}, u32[]{:S(2)}) collective-permute-start(bf16[128,4608]{1,0:T(8,128)(2,1)} %get-tuple-element.15), channel_id=1, source_target_pairs={{8,0},{12,4},{16,8},{20,12},{24,16},{28,20},{9,1},{13,5},{17,9},{2... | collective-permute-start | bytes 3538952 | tf_op jit(solution)/shard_map/ppermute | solution.py:311
  7.7 53.9 %collective-permute-start.2 = (bf16[128,4608]{1,0:T(8,128)(2,1)}, bf16[128,4608]{1,0:T(8,128)(2,1)S(1)}, u32[]{:S(2)}, u32[]{:S(2)}) collective-permute-start(bf16[128,4608]{1,0:T(8,128)(2,1)} %get-tuple-element.16), channel_id=1, source_target_pairs={{8,0},{12,4},{16,8},{20,12},{24,16},{28,20},{9,1},{13,5},{17,9},{2... | collective-permute-start | bytes 3538952 | tf_op jit(solution)/shard_map/ppermute | solution.py:311
  9.7 54.3 %collective-permute-start.7 = (bf16[128,4608]{1,0:T(8,128)(2,1)}, bf16[128,4608]{1,0:T(8,128)(2,1)S(1)}, u32[]{:S(2)}, u32[]{:S(2)}) collective-permute-start(bf16[128,4608]{1,0:T(8,128)(2,1)} %get-tuple-element.15), channel_id=1, source_target_pairs={{0,8},{4,12},{8,16},{12,20},{16,24},{20,28},{1,9},{5,13},{9,17},{1... | collective-permute-start | bytes 3538952 | tf_op jit(solution)/shard_map/ppermute | solution.py:311
  13.6 54.0 %collective-permute-start.8 = (bf16[128,4608]{1,0:T(8,128)(2,1)}, bf16[128,4608]{1,0:T(8,128)(2,1)S(1)}, u32[]{:S(2)}, u32[]{:S(2)}) collective-permute-start(bf16[128,4608]{1,0:T(8,128)(2,1)} %get-tuple-element.16), channel_id=1, source_target_pairs={{0,8},{4,12},{8,16},{12,20},{16,24},{20,28},{1,9},{5,13},{9,17},{1... | collective-permute-start | bytes 3538952 | tf_op jit(solution)/shard_map/ppermute | solution.py:311
  36.4 50.5 %collective-permute-start.3 = (bf16[128,4608]{1,0:T(8,128)(2,1)}, bf16[128,4608]{1,0:T(8,128)(2,1)S(1)}, u32[]{:S(2)}, u32[]{:S(2)}) collective-permute-start(bf16[128,4608]{1,0:T(8,128)(2,1)} %collective-permute-done.1), channel_id=1, source_target_pairs={{8,0},{12,4},{16,8},{20,12},{9,1},{13,5},{17,9},{21,13},{10,2},{14... | collective-permute-start | bytes 3538952 | tf_op jit(solution)/shard_map/ppermute | solution.py:311
  61.6 49.1 %collective-permute-start.4 = (bf16[128,4608]{1,0:T(8,128)(2,1)S(1)}, bf16[128,4608]{1,0:T(8,128)(2,1)S(1)}, u32[]{:S(2)}, u32[]{:S(2)}) collective-permute-start(bf16[128,4608]{1,0:T(8,128)(2,1)S(1)} %collective-permute-done.2), channel_id=1, source_target_pairs={{8,0},{12,4},{16,8},{20,12},{9,1},{13,5},{17,9},{21,13},{10,2},{14... | collective-permute-start | bytes 3538952 | tf_op jit(solution)/shard_map/ppermute | solution.py:311
  64.0 50.6 %collective-permute-start.9 = (bf16[128,4608]{1,0:T(8,128)(2,1)S(1)}, bf16[128,4608]{1,0:T(8,128)(2,1)S(1)}, u32[]{:S(2)}, u32[]{:S(2)}) collective-permute-start(bf16[128,4608]{1,0:T(8,128)(2,1)S(1)} %collective-permute-done.7), channel_id=1, source_target_pairs={{8,16},{12,20},{16,24},{20,28},{9,17},{13,21},{17,25},{21,29},{10,... | collective-permute-start | bytes 3538952 | tf_op jit(solution)/shard_map/ppermute | solution.py:311
  67.6 47.7 %collective-permute-start.10 = (bf16[128,4608]{1,0:T(8,128)(2,1)S(1)}, bf16[128,4608]{1,0:T(8,128)(2,1)S(1)}, u32[]{:S(2)}, u32[]{:S(2)}) collective-permute-start(bf16[128,4608]{1,0:T(8,128)(2,1)S(1)} %collective-permute-done.8), channel_id=1, source_target_pairs={{8,16},{12,20},{16,24},{20,28},{9,17},{13,21},{17,25},{21,29},{10,... | collective-permute-start | bytes 3538952 | tf_op jit(solution)/shard_map/ppermute | solution.py:311
  86.9 48.5 %collective-permute-start.5 = (bf16[128,4608]{1,0:T(8,128)(2,1)S(1)}, bf16[128,4608]{1,0:T(8,128)(2,1)S(1)}, u32[]{:S(2)}, u32[]{:S(2)}) collective-permute-start(bf16[128,4608]{1,0:T(8,128)(2,1)S(1)} %collective-permute-done.3), channel_id=1, source_target_pairs={{8,0},{12,4},{9,1},{13,5},{10,2},{14,6},{11,3},{15,7}} | collective-permute-start | bytes 3538952 | tf_op jit(solution)/shard_map/ppermute | solution.py:311
  110.8 48.5 %collective-permute-start.6 = (bf16[128,4608]{1,0:T(8,128)(2,1)S(1)}, bf16[128,4608]{1,0:T(8,128)(2,1)S(1)}, u32[]{:S(2)}, u32[]{:S(2)}) collective-permute-start(bf16[128,4608]{1,0:T(8,128)(2,1)S(1)} %collective-permute-done.4), channel_id=1, source_target_pairs={{8,0},{12,4},{9,1},{13,5},{10,2},{14,6},{11,3},{15,7}} | collective-permute-start | bytes 3538952 | tf_op jit(solution)/shard_map/ppermute | solution.py:311
  114.6 46.3 %collective-permute-start.11 = (bf16[128,4608]{1,0:T(8,128)(2,1)S(1)}, bf16[128,4608]{1,0:T(8,128)(2,1)S(1)}, u32[]{:S(2)}, u32[]{:S(2)}) collective-permute-start(bf16[128,4608]{1,0:T(8,128)(2,1)S(1)} %collective-permute-done.9), channel_id=1, source_target_pairs={{16,24},{20,28},{17,25},{21,29},{18,26},{22,30},{19,27},{23,31}} | collective-permute-start | bytes 3538952 | tf_op jit(solution)/shard_map/ppermute | solution.py:311
  115.4 45.6 %collective-permute-start.12 = (bf16[128,4608]{1,0:T(8,128)(2,1)S(1)}, bf16[128,4608]{1,0:T(8,128)(2,1)S(1)}, u32[]{:S(2)}, u32[]{:S(2)}) collective-permute-start(bf16[128,4608]{1,0:T(8,128)(2,1)S(1)} %collective-permute-done.10), channel_id=1, source_target_pairs={{16,24},{20,28},{17,25},{21,29},{18,26},{22,30},{19,27},{23,31}} | collective-permute-start | bytes 3538952 | tf_op jit(solution)/shard_map/ppermute | solution.py:311
  185.8 2.9 %collective-permute-start.13 = (bf16[2,4,64,1152]{3,2,1,0:T(8,128)(2,1)S(1)}, bf16[2,4,64,1152]{3,2,1,0:T(8,128)(2,1)S(1)}, u32[]{:S(2)}, u32[]{:S(2)}) collective-permute-start(bf16[2,4,64,1152]{3,2,1,0:T(8,128)(2,1)S(1)} %pad_maximum_fusion.6), channel_id=1, source_target_pairs={{0,1},{1,0},{2,3},{3,2},{4,5},{5,4},{6,7},{7,6},{8,9},{9,8},{10,11... | collective-permute-start | bytes 3538952 | tf_op jit(solution)/shard_map/ppermute | solution.py:314
  189.7 15.7 %collective-permute-start.14 = (bf16[4,64,1152]{2,1,0:T(8,128)(2,1)}, bf16[4,64,1152]{2,1,0:T(8,128)(2,1)}, u32[]{:S(2)}, u32[]{:S(2)}) collective-permute-start(bf16[4,64,1152]{2,1,0:T(8,128)(2,1)} %fusion.1), channel_id=1, source_target_pairs={{0,2},{1,3},{2,0},{3,1},{4,6},{5,7},{6,4},{7,5},{8,10},{9,11},{10,... | collective-permute-start | bytes 1769480 | tf_op jit(solution)/shard_map/ppermute | solution.py:314
  206.7 15.9 %collective-permute-start.15 = (bf16[1,64,1152]{2,1,0:T(8,128)(2,1)S(1)}, bf16[1,64,1152]{2,1,0:T(8,128)(2,1)S(1)}, u32[]{:S(2)}, u32[]{:S(2)}) collective-permute-start(bf16[1,64,1152]{2,1,0:T(8,128)(2,1)S(1)} %get-tuple-element.20), channel_id=1, source_target_pairs={{0,8},{4,12},{8,16},{12,20},{16,24},{20,28},{24,0},{28,4},{1,9},{5... | collective-permute-start | bytes 442376 | tf_op jit(solution)/shard_map/ppermute | solution.py:343
  212.4 12.1 %collective-permute-start.16 = (bf16[1,64,1152]{2,1,0:T(8,128)(2,1)S(1)}, bf16[1,64,1152]{2,1,0:T(8,128)(2,1)S(1)}, u32[]{:S(2)}, u32[]{:S(2)}) collective-permute-start(bf16[1,64,1152]{2,1,0:T(8,128)(2,1)S(1)} %get-tuple-element.19), channel_id=1, source_target_pairs={{0,16},{4,20},{8,24},{12,28},{16,0},{20,4},{24,8},{28,12},{1,17},{... | collective-permute-start | bytes 442376 | tf_op jit(solution)/shard_map/ppermute | solution.py:343
  214.4 12.7 %collective-permute-start.17 = (bf16[1,64,1152]{2,1,0:T(8,128)(2,1)S(1)}, bf16[1,64,1152]{2,1,0:T(8,128)(2,1)S(1)}, u32[]{:S(2)}, u32[]{:S(2)}) collective-permute-start(bf16[1,64,1152]{2,1,0:T(8,128)(2,1)S(1)} %get-tuple-element.18), channel_id=1, source_target_pairs={{0,24},{4,28},{8,0},{12,4},{16,8},{20,12},{24,16},{28,20},{1,25},{... | collective-permute-start | bytes 442376 | tf_op jit(solution)/shard_map/ppermute | solution.py:343
  227.2 15.3 %collective-permute-start.19 = (bf16[4,64,1152]{2,1,0:T(8,128)(2,1)S(1)}, bf16[4,64,1152]{2,1,0:T(8,128)(2,1)S(1)}, u32[]{:S(2)}, u32[]{:S(2)}) collective-permute-start(bf16[4,64,1152]{2,1,0:T(8,128)(2,1)S(1)} %pad_maximum_fusion.7.refs_0_), channel_id=1, source_target_pairs={{0,2},{1,3},{2,0},{3,1},{4,6},{5,7},{6,4},{7,5},{8,10},{9,11},{10,... | collective-permute-start | bytes 1769480 | tf_op jit(solution)/shard_map/ppermute | solution.py:314
  227.8 16.8 %collective-permute-start.18 = (bf16[4,64,1152]{2,1,0:T(8,128)(2,1)S(1)}, bf16[4,64,1152]{2,1,0:T(8,128)(2,1)S(1)}, u32[]{:S(2)}, u32[]{:S(2)}) collective-permute-start(bf16[4,64,1152]{2,1,0:T(8,128)(2,1)S(1)} %pad_maximum_fusion.7.refs_0_), channel_id=1, source_target_pairs={{0,1},{1,0},{2,3},{3,2},{4,5},{5,4},{6,7},{7,6},{8,9},{9,8},{10,11... | collective-permute-start | bytes 1769480 | tf_op jit(solution)/shard_map/ppermute | solution.py:314
  242.6 2.1 collective-permute-start.20
  257.0 3.6 %collective-permute-start.21 = (f32[3]{0:T(128)S(1)}, f32[3]{0:T(128)S(1)}, u32[]{:S(2)}, u32[]{:S(2)}) collective-permute-start(f32[3]{0:T(128)S(1)} %slice_reduce_fusion), channel_id=1, source_target_pairs={{0,4},{4,0},{8,12},{12,8},{16,20},{20,16},{24,28},{28,24},{1,5},{5... | collective-permute-start | bytes 44 | tf_op jit(solution)/shard_map/ppermute | solution.py:361
  260.5 3.6 %collective-permute-start.22 = (f32[3]{0:T(128)S(1)}, f32[3]{0:T(128)S(1)}, u32[]{:S(2)}, u32[]{:S(2)}) collective-permute-start(f32[3]{0:T(128)S(1)} %max.12), channel_id=1, source_target_pairs={{0,8},{4,12},{8,0},{12,4},{16,24},{20,28},{24,16},{28,20},{1,9},{5... | collective-permute-start | bytes 44 | tf_op jit(solution)/shard_map/ppermute | solution.py:361
  264.1 4.5 %collective-permute-start.23 = (f32[3]{0:T(128)S(1)}, f32[3]{0:T(128)S(1)}, u32[]{:S(2)}, u32[]{:S(2)}) collective-permute-start(f32[3]{0:T(128)S(1)} %max.13), channel_id=1, source_target_pairs={{0,16},{4,20},{8,24},{12,28},{16,0},{20,4},{24,8},{28,12},{1,17},{... | collective-permute-start | bytes 44 | tf_op jit(solution)/shard_map/ppermute | solution.py:361
  (9 other events, 153.4 us)
